TPU v7x, 32 devices: a whole 2x2x4 slice. The times are simulated.
32 devices in a mesh: worker: 8 (over y, x, core), mp: 4 (over z).
Axes of the slice: x: 2, y: 2, z: 4, core: 2. Of those that a mesh axis runs over, the one named last changes fastest.
Arguments:
- gradients: float32 [8, 2097152], P('worker', 'mp'), may hold values from -100 to 100
- neighbours: int32 [8, 3], replicated, may hold values from 0 to 7, as said below
- winner: int32 [1], replicated, may hold values from 0 to 7
Outputs:
- scores: float32 [8], replicated
- aggregate: float32 [2097152], P(('mp', 'worker'))
Inputs may be any that keep to these rules, and one draw needn't show every extreme that they name: `neighbours`: row i lists 3 different workers, none of them equal to i.
All inputs are finite; a program needn't handle non-finite values.
Results may differ from a plain program's by a relative error of at most 0.0003.
Values may be sent and summed in bfloat16 or wider, within the bound.
No kernel may reach another device: no remote copies, remote signals or barrier semaphores. Data moves between devices by JAX's collectives and lax.ppermute only.
A program may use at most 64 MiB of HBM per device.

v0:
```python
import jax
import jax.numpy as jnp
from jax import lax
from jax.sharding import PartitionSpec as P


def from_root(block, axis, holder):
    block = jnp.where(lax.axis_index(axis) == holder, block, jnp.zeros_like(block))
    return lax.psum(block, axis)


def body(gradients, neighbours, winner):
    rounded = gradients.astype(jnp.bfloat16)
    workers = lax.axis_size("worker")
    own_index = lax.axis_index("worker")
    length = gradients.shape[1]
    columns = lax.all_to_all(rounded, "worker", split_axis=1, concat_axis=0, tiled=True)
    partial_value = lax.dot_general(
        columns, columns, (((1,), (1,)), ((), ())), preferred_element_type=jnp.float32
    )
    gram_matrix = lax.psum(partial_value, ("worker", "mp"))
    squares = jnp.diagonal(gram_matrix)
    distance = squares[:, None] + squares[None, :] - 2.0 * gram_matrix
    counts = jnp.sum(
        (neighbours[:, :, None] == jnp.arange(workers, dtype=jnp.int32)[None, None, :]).astype(
            jnp.float32
        ),
        axis=1,
    )
    total_entries = neighbours.shape[1] * length * lax.axis_size("mp")
    scores = jnp.sum(counts * distance, axis=1) / jnp.float32(total_entries)
    piece_length = length // workers
    selected = from_root(gradients[0], "worker", winner[0])
    aggregate = lax.dynamic_slice_in_dim(selected, own_index * piece_length, piece_length, 0)
    return (scores, aggregate)


def solution(mesh):
    in_specs = (P("worker", "mp"), P(), P())
    out_specs = (P(), P(("mp", "worker")))
    return jax.shard_map(body, mesh=mesh, in_specs=in_specs, out_specs=out_specs, check_vma=False)
```

profile of v0, /device:TPU:0, one launch (start us, length us, event | category | flops | bytes accessed | tf_op | source)
XLA Modules:
  0.0 107.3 jit_solution(818342998343869056)
XLA Ops:
  7.8 6.5 %broadcast_select_fusion = (f32[1,524288]{1,0:T(1,128)}, bf16[1,524288]{1,0:T(2,128)(2,1)S(1)}) fusion(f32[1,524288]{1,0:T(1,128)} %param.3, pred[]{:T(512)S(6)} %eq.19), kind=kLoop, calls=%fused_computation.1 | loop fusion | flops 1048576 | bytes 5242881 | tf_op jit(solution)/shard_map/jit(_where)/select_n | solution.py:8
  14.3 0.5 broadcast.34
  14.8 7.0 %reduce = bf16[8,65536]{1,0:T(8,128)(2,1)S(1)} reduce(bf16[8,1,65536]{2,1,0:T(2,128)(2,1)S(1)} %bitcast.12, bf16[]{:T(256)} %broadcast.34), dimensions={1}, to_apply=%bitcast.8.reduce_sub_computation | reduce | bytes 2097154
  21.9 1.9 %reshape.22 = bf16[8,2,32768]{2,1,0:T(2,128)(2,1)} reshape(bf16[8,65536]{1,0:T(8,128)(2,1)S(1)} %reduce) | data formatting | bytes 2097152
  23.7 0.0 copy-start
  23.7 5.3 %all-to-all-start = ((bf16[8,2,32768]{2,1,0:T(2,128)(2,1)}), bf16[8,2,32768]{2,1,0:T(2,128)(2,1)S(1)}, u32[]{:S(2)}, u32[]{:S(2)}) async-start(bf16[8,2,32768]{2,1,0:T(2,128)(2,1)} %reshape.22), calls=%async_computation | async-start | bytes 2097152 | tf_op jit(solution)/shard_map/all_to_all | solution.py:17
  29.1 0.0 all-reduce.2.cloned.1.call-start
  29.1 0.7 all-reduce.2.cloned.1.call-update
  29.8 0.0 copy-done
  29.8 0.1 convert_reduce_fusion
  29.9 16.4 %all-to-all-done = bf16[8,2,32768]{2,1,0:T(2,128)(2,1)S(1)} async-done(((bf16[8,2,32768]{2,1,0:T(2,128)(2,1)}), bf16[8,2,32768]{2,1,0:T(2,128)(2,1)S(1)}, u32[]{:S(2)}, u32[]{:S(2)}) %all-to-all-start) | async-done | bytes 1048608 | tf_op jit(solution)/shard_map/all_to_all | solution.py:17
  46.3 1.0 reshape.23
  47.3 1.2 %fusion = f32[8,8]{1,0:T(8,128)S(1)} fusion(bf16[1,8,65536]{2,0,1:T(2,128)(2,1)S(1)} %bitcast.13), kind=kOutput, calls=%fused_computation.2 | convolution fusion | flops 8388608 | bytes 1048832 | tf_op jit(solution)/shard_map/dot_general | solution.py:18
  48.5 39.8 %psum.14 = f32[8,8]{1,0:T(8,128)S(1)} all-reduce(f32[8,8]{1,0:T(8,128)S(1)} %fusion), channel_id=1, replica_groups=mesh['worker'=8,'mp'=4] {'worker','mp'}, use_global_device_ids=true, to_apply=%region_1.2 | all-reduce | flops 64 | bytes 512 | tf_op jit(solution)/shard_map/psum | solution.py:21
  88.3 0.6 gather_fusion
  88.9 0.2 multiply_reduce_fusion
  89.1 0.5 broadcast_multiply_fusion
  89.6 9.1 %all-reduce.2.cloned.1.call-done = f32[524288]{0:T(1024)} async-done(((f32[524288]{0:T(1024)}), f32[524288]{0:T(1024)}) %all-reduce.2.cloned.1.call-update) | async-done | bytes 2097168 | tf_op jit(solution)/shard_map/psum | solution.py:9
  98.8 1.7 %dynamic_slice.3 = f32[65536]{0:T(1024)} dynamic-slice(f32[524288]{0:T(1024)} %all-reduce.2.cloned.1.call-done, s32[]{:T(128)S(6)} %select_n.21), dynamic_slice_sizes={65536} | dynamic-slice | bytes 524292 | tf_op jit(solution)/shard_map/dynamic_slice | solution.py:34
  (1 shorter events, 0.0 us)
Async XLA Ops:
  23.7 6.1 %copy-start = (s32[8,3]{0,1:T(4,128)S(1)}, s32[8,3]{0,1:T(4,128)}, u32[]{:S(2)}) copy-start(s32[8,3]{0,1:T(4,128)} %param.4) | copy-start | bytes 292
  23.7 22.5 %all-to-all-start = ((bf16[8,2,32768]{2,1,0:T(2,128)(2,1)}), bf16[8,2,32768]{2,1,0:T(2,128)(2,1)S(1)}, u32[]{:S(2)}, u32[]{:S(2)}) async-start(bf16[8,2,32768]{2,1,0:T(2,128)(2,1)} %reshape.22), calls=%async_computation | async-start | bytes 2097152 | tf_op jit(solution)/shard_map/all_to_all | solution.py:17
  29.1 69.7 %all-reduce.2.cloned.1.call-start = ((), (), s32[]{:S(2)}) async-start(), calls=%async_computation.1 | async-start | bytes 4194304 | tf_op jit(solution)/shard_map/psum | solution.py:9
Sparse Core Ops, SparseCore 0:
  33.1 65.6 all-reduce.1
where the time goes:
time: 108 us; the launch traced here: 107 us
  blocking collectives  39.8 us (37%)
  waiting for transfers between devices  26.2 us (24%)
  between operations  14.7 us (14%)
  other arithmetic  14.3 us (13%)
  local copies, waits for them, and re-layouts  5.71 us (5%)
  starting transfers between devices  5.37 us (5%)
  matrix products  1.2 us (1%)
    psum x1, blocking collectives, body(): gram_matrix = lax.psum(partial_value, ('worker', 'mp'))  39.8 us
    all_to_all x1, waiting for transfers between devices, body(): lax.all_to_all(rounded, 'worker', split_axis=1, concat_axis=0, tiled=True)  16.4 us
    psum x1, waiting for transfers between devices, from_root(): return lax.psum(block, axis)  9.12 us
    unnamed x1, other arithmetic  7.03 us
    select_n x1, other arithmetic, from_root(): jnp.where(lax.axis_index(axis) == holder, block, jnp.zeros_like(block))  6.5 us
    all_to_all x1, starting transfers between devices, body(): lax.all_to_all(rounded, 'worker', split_axis=1, concat_axis=0, tiled=True)  5.33 us
    unnamed x5, local copies, waits for them, and re-layouts  3.41 us
  transfers between devices with their start and end apart: 2, of which 2 were waited for; matrix products, arithmetic and copies ran while one was open for 3% of the time, Pallas kernels for 0%

commit v1 on v0

--- a/solution.py
+++ b/solution.py
@@ -2,6 +2,7 @@
 import jax.numpy as jnp
 from jax import lax
 from jax.sharding import PartitionSpec as P
+from jax.lax import all_gather
 
 
 def from_root(block, axis, holder):
@@ -18,7 +19,8 @@
     partial_value = lax.dot_general(
         columns, columns, (((1,), (1,)), ((), ())), preferred_element_type=jnp.float32
     )
-    gram_matrix = lax.psum(partial_value, ("worker", "mp"))
+    manage_words = lambda block_in: all_gather(block_in, ("worker", "mp")).sum(axis=0)
+    gram_matrix = manage_words(partial_value)
     squares = jnp.diagonal(gram_matrix)
     distance = squares[:, None] + squares[None, :] - 2.0 * gram_matrix
     counts = jnp.sum(

time: 108 us -> 126 us (1.17)
  blocking collectives: 39.8 us -> 67.3 us
  waiting for transfers between devices: 26.2 us -> 17 us
    all_gather x0 -> x1, blocking collectives: none -> 67.3 us  [body(): all_gather(block_in, ('worker', 'mp')).sum(axis=0)]
    psum x1 -> x0, blocking collectives: 39.8 us -> none  [body(): gram_matrix = lax.psum(partial_value, ('worker', 'mp'))]
    psum x1, waiting for transfers between devices: 9.12 us -> 0.01 us  [from_root(): return lax.psum(block, axis)]
  transfers between devices with their start and end apart: 2 -> 2, of which waited for: 2 -> 1; matrix products, arithmetic and copies ran while one was open for 3% -> 3% of each run, Pallas kernels for 0% -> 0%
where the time goes in v1:
time: 126 us
  blocking collectives  67.3 us (53%)
  waiting for transfers between devices  17 us (13%)
  between operations  14.7 us (12%)
  other arithmetic  14.3 us (11%)
  local copies, waits for them, and re-layouts  5.71 us (5%)
  starting transfers between devices  5.37 us (4%)
    all_gather x1, blocking collectives, body(): all_gather(block_in, ('worker', 'mp')).sum(axis=0)  67.3 us
    all_to_all x1, waiting for transfers between devices, body(): lax.all_to_all(rounded, 'worker', split_axis=1, concat_axis=0, tiled=True)  16.4 us
    unnamed x1, other arithmetic  7.03 us
    select_n x1, other arithmetic, from_root(): jnp.where(lax.axis_index(axis) == holder, block, jnp.zeros_like(block))  6.49 us
    all_to_all x1, starting transfers between devices, body(): lax.all_to_all(rounded, 'worker', split_axis=1, concat_axis=0, tiled=True)  5.33 us
    unnamed x5, local copies, waits for them, and re-layouts  3.41 us
  transfers between devices with their start and end apart: 2, of which 1 were waited for; matrix products, arithmetic and copies ran while one was open for 3% of the time, Pallas kernels for 0%

profile of v1, /device:TPU:0, one launch (start us, length us, event | category | flops | bytes accessed | tf_op | source)
XLA Modules:
  0.0 125.7 jit_solution(11120278656684225482)
XLA Ops:
  7.8 6.5 %broadcast_select_fusion = (f32[1,524288]{1,0:T(1,128)}, bf16[1,524288]{1,0:T(2,128)(2,1)S(1)}) fusion(f32[1,524288]{1,0:T(1,128)} %param.3, pred[]{:T(512)S(6)} %eq.19), kind=kLoop, calls=%fused_computation.1 | loop fusion | flops 1048576 | bytes 5242881 | tf_op jit(solution)/shard_map/jit(_where)/select_n | solution.py:9
  14.3 0.5 broadcast.34
  14.8 7.0 %reduce = bf16[8,65536]{1,0:T(8,128)(2,1)S(1)} reduce(bf16[8,1,65536]{2,1,0:T(2,128)(2,1)S(1)} %bitcast.14, bf16[]{:T(256)} %broadcast.34), dimensions={1}, to_apply=%bitcast.10.reduce_sub_computation | reduce | bytes 2097154
  21.9 1.9 %reshape.23 = bf16[8,2,32768]{2,1,0:T(2,128)(2,1)} reshape(bf16[8,65536]{1,0:T(8,128)(2,1)S(1)} %reduce) | data formatting | bytes 2097152
  23.7 0.0 copy-start
  23.7 5.3 %all-to-all-start = ((bf16[8,2,32768]{2,1,0:T(2,128)(2,1)}), bf16[8,2,32768]{2,1,0:T(2,128)(2,1)S(1)}, u32[]{:S(2)}, u32[]{:S(2)}) async-start(bf16[8,2,32768]{2,1,0:T(2,128)(2,1)} %reshape.23), calls=%async_computation | async-start | bytes 2097152 | tf_op jit(solution)/shard_map/all_to_all | solution.py:18
  29.1 0.0 all-reduce.2.cloned.1.call-start
  29.1 0.7 all-reduce.2.cloned.1.call-update
  29.8 0.0 copy-done
  29.8 0.1 convert_reduce_fusion
  29.9 16.4 %all-to-all-done = bf16[8,2,32768]{2,1,0:T(2,128)(2,1)S(1)} async-done(((bf16[8,2,32768]{2,1,0:T(2,128)(2,1)}), bf16[8,2,32768]{2,1,0:T(2,128)(2,1)S(1)}, u32[]{:S(2)}, u32[]{:S(2)}) %all-to-all-start) | async-done | bytes 1048608 | tf_op jit(solution)/shard_map/all_to_all | solution.py:18
  46.2 1.0 reshape.24
  47.3 1.2 fusion
  48.5 67.3 %all-gather = f32[256,8]{1,0:T(8,128)S(1)} all-gather(f32[8,8]{1,0:T(8,128)S(1)} %fusion), channel_id=2, replica_groups=mesh['worker'=8,'mp'=4] {'worker','mp'}, dimensions={0}, use_global_device_ids=true | all-gather | bytes 8448 | tf_op jit(solution)/shard_map/all_gather | solution.py:22
  115.8 0.6 gather_fusion
  116.5 0.2 multiply_reduce_fusion
  116.7 0.5 broadcast_multiply_fusion
  117.2 0.0 all-reduce.2.cloned.1.call-done
  117.2 1.7 %dynamic_slice.3 = f32[65536]{0:T(1024)} dynamic-slice(f32[524288]{0:T(1024)} %all-reduce.2.cloned.1.call-done, s32[]{:T(128)S(6)} %select_n.21), dynamic_slice_sizes={65536} | dynamic-slice | bytes 524292 | tf_op jit(solution)/shard_map/dynamic_slice | solution.py:36
  (2 shorter events, 0.0 us)
Async XLA Ops:
  23.7 6.1 %copy-start = (s32[8,3]{0,1:T(4,128)S(1)}, s32[8,3]{0,1:T(4,128)}, u32[]{:S(2)}) copy-start(s32[8,3]{0,1:T(4,128)} %param.4) | copy-start | bytes 292
  23.7 22.5 %all-to-all-start = ((bf16[8,2,32768]{2,1,0:T(2,128)(2,1)}), bf16[8,2,32768]{2,1,0:T(2,128)(2,1)S(1)}, u32[]{:S(2)}, u32[]{:S(2)}) async-start(bf16[8,2,32768]{2,1,0:T(2,128)(2,1)} %reshape.23), calls=%async_computation | async-start | bytes 2097152 | tf_op jit(solution)/shard_map/all_to_all | solution.py:18
  29.1 88.1 %all-reduce.2.cloned.1.call-start = ((), (), s32[]{:S(2)}) async-start(), calls=%async_computation.1 | async-start | bytes 4194304 | tf_op jit(solution)/shard_map/psum | solution.py:10
Sparse Core Ops, SparseCore 0:
  33.1 65.4 all-reduce.1
